TPU v7x, 32 devices: a whole 2x2x4 slice. The times are simulated.
32 devices in a mesh: zero: 4 (over z), model: 4 (over x, core), trial: 2 (over y).
Axes of the slice: x: 2, y: 2, z: 4, core: 2. Of those that a mesh axis runs over, the one named last changes fastest.
Arguments:
- w_query: bfloat16 [4096, 2048], P(('trial', 'zero'), 'model'), parts along dimension 0, may hold values from -0.125 to 0.125
- low_query: bfloat16 [4096, 32], P(('trial', 'zero')), parts along dimension 0, may hold values from -0.125 to 0.125
- high_query: bfloat16 [64, 2048], P('trial', 'model'), parts along dimension 0, may hold values from -1 to 1
- w_key: bfloat16 [4096, 512], P(('trial', 'zero'), 'model'), parts along dimension 0, may hold values from -0.125 to 0.125
- low_key: bfloat16 [4096, 32], P(('trial', 'zero')), parts along dimension 0, may hold values from -0.125 to 0.125
- high_key: bfloat16 [64, 512], P('trial', 'model'), parts along dimension 0, may hold values from -1 to 1
- w_value: bfloat16 [4096, 512], P(('trial', 'zero'), 'model'), parts along dimension 0, may hold values from -0.125 to 0.125
- low_value: bfloat16 [4096, 32], P(('trial', 'zero')), parts along dimension 0, may hold values from -0.125 to 0.125
- high_value: bfloat16 [64, 512], P('trial', 'model'), parts along dimension 0, may hold values from -1 to 1
- w_mixed: bfloat16 [4096, 2048], P(('trial', 'model'), 'zero'), parts along dimension 0, may hold values from -0.125 to 0.125
- low_mixed: bfloat16 [4096, 32], P(('trial', 'model')), parts along dimension 0, may hold values from -0.125 to 0.125
- high_mixed: bfloat16 [64, 2048], P('trial', 'zero'), parts along dimension 0, may hold values from -1 to 1
- norm_train: float32 [4096], P(('trial', 'zero', 'model')), parts along dimension 0, may hold values from 0.25 to 1.75
- norm_step: float32 [4096], P(('trial', 'zero', 'model')), parts along dimension 0, may hold values from -0.3 to 0.3
Outputs:
- final_query: bfloat16 [4096, 2048], P('trial', 'model'), parts along dimension 0
- final_key: bfloat16 [4096, 512], P('trial', 'model'), parts along dimension 0
- final_value: bfloat16 [4096, 512], P('trial', 'model'), parts along dimension 0
- final_mixed: bfloat16 [4096, 2048], P(('trial', 'model')), parts along dimension 0
- serve_norm: bfloat16 [4096], P('trial'), parts along dimension 0
There are 2 independent parts, one for each index of `trial`. A program takes and returns all parts, laid end to end along the dimension named above; each array names one. Nothing has to cross between parts.
All inputs are finite; a program needn't handle non-finite values.
Results may differ from a plain program's by a relative error of at most 0.001.
Values may be sent and summed in bfloat16 or wider, within the bound.
A program may use at most 64 MiB of HBM per device.

v0:
```python
import jax
import jax.numpy as jnp
from jax import lax
from jax.sharding import PartitionSpec as P

mix_rate = 2.0


def shards(
    w_query,
    low_query,
    high_query,
    w_key,
    low_key,
    high_key,
    w_value,
    low_value,
    high_value,
    w_mixed,
    low_mixed,
    high_mixed,
    norm_train,
    norm_step,
):
    result_query = w_query.astype(jnp.float32) + mix_rate * jnp.dot(
        low_query, high_query, preferred_element_type=jnp.float32
    )
    result_key = w_key.astype(jnp.float32) + mix_rate * jnp.dot(
        low_key, high_key, preferred_element_type=jnp.float32
    )
    result_value = w_value.astype(jnp.float32) + mix_rate * jnp.dot(
        low_value, high_value, preferred_element_type=jnp.float32
    )
    result_mixed = w_mixed.astype(jnp.float32) + mix_rate * jnp.dot(
        low_mixed, high_mixed, preferred_element_type=jnp.float32
    )
    narrow_query, narrow_key, narrow_value, narrow_mixed = (
        result_query.astype(jnp.bfloat16),
        result_key.astype(jnp.bfloat16),
        result_value.astype(jnp.bfloat16),
        result_mixed.astype(jnp.bfloat16),
    )
    final_query, final_key, final_value, final_mixed = (
        lax.all_gather(narrow_query, "zero", axis=0, tiled=True),
        lax.all_gather(narrow_key, "zero", axis=0, tiled=True),
        lax.all_gather(narrow_value, "zero", axis=0, tiled=True),
        lax.all_gather(narrow_mixed, "zero", axis=1, tiled=True),
    )
    serve_norm = lax.all_gather(
        (norm_train + norm_step).astype(jnp.bfloat16), ("zero", "model"), axis=0, tiled=True
    )
    return (final_query, final_key, final_value, final_mixed, serve_norm)


def solution(mesh):
    placed = (
        P(("trial", "zero"), "model"),
        P(("trial", "zero"), None),
        P("trial", "model"),
        P(("trial", "zero"), "model"),
        P(("trial", "zero"), None),
        P("trial", "model"),
        P(("trial", "zero"), "model"),
        P(("trial", "zero"), None),
        P("trial", "model"),
        P(("trial", "model"), "zero"),
        P(("trial", "model"), None),
        P("trial", "zero"),
        P(("trial", "zero", "model")),
        P(("trial", "zero", "model")),
    )
    return jax.shard_map(
        shards,
        mesh=mesh,
        in_specs=placed,
        out_specs=(
            P("trial", "model"),
            P("trial", "model"),
            P("trial", "model"),
            P(("trial", "model"), None),
            P("trial"),
        ),
        check_vma=False,
    )
```

profile of v0, /device:TPU:0, one launch (start us, length us, event | category | flops | bytes accessed | tf_op | source)
XLA Modules:
  0.0 131.7 jit_solution(212639038545267897)
XLA Ops:
  7.2 0.0 copy-start
  7.2 0.0 copy-start.2
  7.2 0.0 copy-start.4
  7.2 0.0 copy-start.6
  7.2 0.0 copy-start.3
  7.2 0.0 copy-start.5
  7.2 0.0 copy-start.7
  7.2 0.0 all-gather.4.cloned.1.call-start
  7.3 0.6 copy-done
  7.9 2.2 %fusion.2 = bf16[512,512]{1,0:T(8,128)(2,1)} fusion(bf16[512,32]{0,1:T(8,128)(2,1)S(1)} %copy-done, bf16[32,512]{1,0:T(8,128)(2,1)} %param.16, bf16[512,512]{1,0:T(8,128)(2,1)} %param.14), kind=kOutput, calls=%fused_computation.4 | convolution fusion | flops 17825792 | bytes 1114112 | tf_op jit(solution)/shard_map/dot_general | solution.py:25
  10.1 0.0 copy-start.8
  10.1 0.0 copy-start.9
  10.1 0.0 all-gather.4.cloned.1.call-update
  10.1 0.0 all-gather.6.cloned.1.call-start
  10.2 2.2 %fusion.3 = bf16[512,512]{1,0:T(8,128)(2,1)} fusion(bf16[512,32]{0,1:T(8,128)(2,1)} %param.24, bf16[32,512]{1,0:T(8,128)(2,1)} %param.25, bf16[512,512]{1,0:T(8,128)(2,1)} %param.23), kind=kOutput, calls=%fused_computation.5 | convolution fusion | flops 17825792 | bytes 1114112 | tf_op jit(solution)/shard_map/dot_general | solution.py:34
  12.4 0.0 all-gather.6.cloned.1.call-update
  12.4 0.0 copy-done.2
  12.4 0.0 copy-done.4
  12.4 0.0 copy-done.6
  12.4 0.2 fusion.6
  12.7 23.1 %all_gather.16 = bf16[2048,128]{1,0:T(8,128)(2,1)S(1)} all-gather(bf16[512,128]{1,0:T(8,128)(2,1)S(1)} %fusion.6), channel_id=1, replica_groups=mesh['zero'=4,'model'=4,'trial'=2] {'zero'}, dimensions={0}, use_global_device_ids=true | all-gather | bytes 655360 | tf_op jit(solution)/shard_map/all_gather | solution.py:45
  35.8 0.0 copy-done.3
  35.8 0.0 copy-done.5
  35.8 0.0 copy-done.7
  35.8 0.2 fusion.7
  36.0 21.4 %all_gather.17 = bf16[2048,128]{1,0:T(8,128)(2,1)S(1)} all-gather(bf16[512,128]{1,0:T(8,128)(2,1)S(1)} %fusion.7), channel_id=1, replica_groups=mesh['zero'=4,'model'=4,'trial'=2] {'zero'}, dimensions={0}, use_global_device_ids=true | all-gather | bytes 655360 | tf_op jit(solution)/shard_map/all_gather | solution.py:46
  57.4 0.0 copy-done.8
  57.4 0.0 copy-done.9
  57.4 20.5 %all-gather = bf16[16,1,128]{2,1,0:T(2,128)(2,1)S(1)} all-gather(bf16[1,1,128]{2,1,0:T(2,128)(2,1)S(1)} %convert_bitcast_fusion), channel_id=1, replica_groups=mesh['zero'=4,'model'=4,'trial'=2] {'zero','model'}, dimensions={0}, use_global_device_ids=true | all-gather | bytes 4352 | tf_op jit(solution)/shard_map/all_gather | solution.py:49
  77.9 0.6 reduce
  78.5 0.0 all-gather.4.cloned.1.call-done
  78.5 40.3 %all-gather.6.cloned.1.call-done = bf16[512,2048]{1,0:T(8,128)(2,1)} async-done(((bf16[512,512]{1,0:T(8,128)(2,1)}), bf16[512,2048]{1,0:T(8,128)(2,1)}) %all-gather.6.cloned.1.call-update) | async-done | bytes 2097168 | tf_op jit(solution)/shard_map/all_gather | solution.py:47
  118.8 0.0 copy-start.1
  118.8 3.2 %copy.23 = bf16[2048,512]{1,0:T(8,128)(2,1)} copy(bf16[2048,512]{1,0:T(8,128)(2,1)} %all-gather.4.cloned.1.call-done) | data formatting | bytes 4194304
  122.0 0.8 copy.24
  122.8 0.8 copy.25
  123.6 0.0 copy-done.1
  123.6 1.3 %copy.26 = bf16[512,2048]{1,0:T(8,128)(2,1)} copy(bf16[512,2048]{1,0:T(8,128)(2,1)S(1)} %copy-done.1) | data formatting | bytes 4194304
  (1 shorter events, 0.0 us)
Async XLA Ops:
  7.2 0.8 copy-start
  7.2 5.2 %copy-start.2 = (bf16[512,128]{1,0:T(8,128)(2,1)S(1)}, bf16[512,128]{1,0:T(8,128)(2,1)}, u32[]{:S(2)}) copy-start(bf16[512,128]{1,0:T(8,128)(2,1)} %param.17) | copy-start | bytes 393220
  7.2 5.2 %copy-start.4 = (bf16[512,32]{0,1:T(8,128)(2,1)S(1)}, bf16[512,32]{0,1:T(8,128)(2,1)}, u32[]{:S(2)}) copy-start(bf16[512,32]{0,1:T(8,128)(2,1)} %param.18) | copy-start | bytes 98308
  7.2 5.2 %copy-start.6 = (bf16[32,128]{1,0:T(8,128)(2,1)S(1)}, bf16[32,128]{1,0:T(8,128)(2,1)}, u32[]{:S(2)}) copy-start(bf16[32,128]{1,0:T(8,128)(2,1)} %param.19) | copy-start | bytes 24580
  7.2 28.6 %copy-start.3 = (bf16[512,128]{1,0:T(8,128)(2,1)S(1)}, bf16[512,128]{1,0:T(8,128)(2,1)}, u32[]{:S(2)}) copy-start(bf16[512,128]{1,0:T(8,128)(2,1)} %param.20) | copy-start | bytes 393220
  7.2 28.6 %copy-start.5 = (bf16[512,32]{0,1:T(8,128)(2,1)S(1)}, bf16[512,32]{0,1:T(8,128)(2,1)}, u32[]{:S(2)}) copy-start(bf16[512,32]{0,1:T(8,128)(2,1)} %param.21) | copy-start | bytes 98308
  7.2 28.5 %copy-start.7 = (bf16[32,128]{1,0:T(8,128)(2,1)S(1)}, bf16[32,128]{1,0:T(8,128)(2,1)}, u32[]{:S(2)}) copy-start(bf16[32,128]{1,0:T(8,128)(2,1)} %param.22) | copy-start | bytes 24580
  7.2 71.2 %all-gather.4.cloned.1.call-start = ((), (), s32[]{:S(2)}) async-start(), calls=%async_computation | async-start | bytes 2621440 | tf_op jit(solution)/shard_map/all_gather | solution.py:44
  10.1 47.3 %copy-start.8 = (f32[128]{0:T(128)S(1)}, f32[128]{0:T(128)}, u32[]{:S(2)}) copy-start(f32[128]{0:T(128)} %param.26) | copy-start | bytes 1540
  10.1 47.3 %copy-start.9 = (f32[128]{0:T(128)S(1)}, f32[128]{0:T(128)}, u32[]{:S(2)}) copy-start(f32[128]{0:T(128)} %param.27) | copy-start | bytes 1540
  10.1 108.7 %all-gather.6.cloned.1.call-start = ((), (), s32[]{:S(2)}) async-start(), calls=%async_computation.1 | async-start | bytes 2621440 | tf_op jit(solution)/shard_map/all_gather | solution.py:47
  118.8 4.8 %copy-start.1 = (bf16[512,2048]{1,0:T(8,128)(2,1)S(1)}, bf16[512,2048]{1,0:T(8,128)(2,1)}, u32[]{:S(2)}) copy-start(bf16[512,2048]{1,0:T(8,128)(2,1)} %all-gather.6.cloned.1.call-done) | copy-start | bytes 6291460
Sparse Core Ops, SparseCore 0:
  10.3 60.5 all-gather.3
  73.0 45.7 all-gather.5
where the time goes:
time: 132 us
  blocking collectives  65 us (49%)
  waiting for transfers between devices  40.3 us (31%)
  between operations  14.2 us (11%)
  local copies, waits for them, and re-layouts  6.78 us (5%)
  matrix products  4.8 us (4%)
    all_gather x1, waiting for transfers between devices, shards(): lax.all_gather(narrow_mixed, 'zero', axis=1, tiled=True)  40.3 us
    all_gather x1, blocking collectives, shards(): lax.all_gather(narrow_key, 'zero', axis=0, tiled=True)  23.1 us
    all_gather x1, blocking collectives, shards(): lax.all_gather(narrow_value, 'zero', axis=0, tiled=True)  21.4 us
    all_gather x1, blocking collectives, shards(): lax.all_gather((norm_train + norm_step).astype(jnp.bfloat16), ('zero', 'm...  20.5 us
    unnamed x24, local copies, waits for them, and re-layouts  6.78 us
  transfers between devices with their start and end apart: 2, of which 1 were waited for; matrix products, arithmetic and copies ran while one was open for 2% of the time, Pallas kernels for 0%

commit v1 on v0

v1 whole, which is shorter than its diff:
```python
import functools

import jax
import jax.numpy as jnp
from jax import lax
from jax.experimental import pallas as pl
from jax.experimental.pallas import tpu as pltpu
from jax.sharding import PartitionSpec as P

MESH = pl.DeviceIdType.MESH
mix_rate = 2.0
piece_rows = 128


def merge_and_gather(zeros, models, *refs):
    (w_q, low_q, high_q, w_k, low_k, high_k, w_v, low_v, high_v, w_m, low_m, high_m) = refs[:12]
    train, step = refs[12:14]
    out_q, out_k, out_v, out_m, out_n = refs[14:19]
    held = refs[19:33]
    load_sem, send_sem, recv_sem, row_send, row_recv = refs[33:]

    z = lax.axis_index("zero")
    m = lax.axis_index("model")
    has_right, has_left = z < zeros - 1, z > 0

    loads = []
    for i in (1, 2, 0, 12, 13, 4, 5, 3, 7, 8, 6, 10, 11, 9):
        copy = pltpu.make_async_copy(refs[i], held[i], load_sem.at[i])
        copy.start()
        loads.append((i, copy))
    loads = dict(loads)

    barrier = pltpu.get_barrier_semaphore()

    @pl.when(has_right)
    def _():
        pl.semaphore_signal(barrier, inc=1, device_id={"zero": z + 1}, device_id_type=MESH)

    @pl.when(has_left)
    def _():
        pl.semaphore_signal(barrier, inc=1, device_id={"zero": z - 1}, device_id_type=MESH)

    for d in range(1, models):
        pl.semaphore_signal(
            barrier, inc=1, device_id={"model": lax.rem(m + d, models)}, device_id_type=MESH
        )

    pieces = []

    def rows_of(out, w):
        rows = w.shape[0]
        size = min(piece_rows, rows)
        return [(out, w, first, size) for first in range(0, rows, size)]

    groups = []
    for position, (out, w) in enumerate(((out_q, w_q), (out_k, w_k), (out_v, w_v), (out_m, w_m))):
        own = rows_of(out, w)
        groups.append((position, len(pieces), own))
        pieces += own
    count = len(pieces) + 1

    def view(shard, c):
        if c == count - 1:
            return out_n.at[shard]
        out, w, first, size = pieces[c]
        rows, columns = w.shape
        if out is out_m:
            return out.at[pl.ds(first, size), pl.ds(pl.multiple_of(shard * columns, columns), columns)]
        return out.at[pl.ds(pl.multiple_of(shard * rows + first, size), size), :]

    def hop(shard, c, way):
        return pltpu.make_async_remote_copy(
            src_ref=view(shard, c),
            dst_ref=view(shard, c),
            send_sem=send_sem.at[way, shard, c],
            recv_sem=recv_sem.at[shard, c],
            device_id={"zero": z + 1 if way == 0 else z - 1},
            device_id_type=MESH,
        )

    def send_own(c):
        @pl.when(has_right)
        def _():
            hop(z, c, 0).start()

        @pl.when(has_left)
        def _():
            hop(z, c, 1).start()

    ready = []
    waited = False
    for position, base, own in groups:
        for i in (1, 2, 0):
            loads[3 * position + i].wait()
        w, low, high = held[3 * position : 3 * position + 3]
        for j, (out, _, first, size) in enumerate(own):
            product = lax.dot_general(
                low[:, first : first + size],
                high[...],
                (((0,), (0,)), ((), ())),
                preferred_element_type=jnp.float32,
            )
            merged = w[first : first + size, :].astype(jnp.float32) + mix_rate * product
            view(z, base + j)[...] = merged.astype(out.dtype)
            ready.append(base + j)
        if position == 0:
            loads[12].wait()
            loads[13].wait()
            out_n[z, m] = held[12][...] + held[13][...]
            pl.semaphore_wait(
                barrier, models - 1 + has_right.astype(jnp.int32) + has_left.astype(jnp.int32)
            )
        while len(ready) > 1:
            send_own(ready.pop(0))
    send_own(ready.pop(0))

    def row(d):
        return pltpu.make_async_remote_copy(
            src_ref=out_n.at[z, m],
            dst_ref=out_n.at[z, m],
            send_sem=row_send.at[d],
            recv_sem=row_recv.at[d],
            device_id={"model": lax.rem(m + d, models)},
            device_id_type=MESH,
        )

    def row_from(d):
        sender = lax.rem(m + models - d, models)
        return pltpu.make_async_remote_copy(
            src_ref=out_n.at[z, sender],
            dst_ref=out_n.at[z, sender],
            send_sem=row_send.at[d],
            recv_sem=row_recv.at[d],
            device_id={"model": sender},
            device_id_type=MESH,
        )

    for d in range(1, models):
        row(d).start()
    for d in range(1, models):
        row_from(d).wait_recv()
    send_own(count - 1)

    def pass_on(k, carry):
        from_left, from_right = z - 1 - k, z + 1 + k
        for c in range(count):

            @pl.when(from_left >= 0)
            def _():
                hop(from_left, c, 0).wait_recv()

                @pl.when(has_right)
                def _():
                    hop(from_left, c, 0).start()

            @pl.when(from_right < zeros)
            def _():
                hop(from_right, c, 1).wait_recv()

                @pl.when(has_left)
                def _():
                    hop(from_right, c, 1).start()

        return carry

    lax.fori_loop(0, zeros - 1, pass_on, 0)

    for d in range(1, models):
        row(d).wait_send()

    def drain(k, carry):
        for c in range(count):

            @pl.when(jnp.logical_and(has_right, z - k >= 0))
            def _():
                hop(z - k, c, 0).wait_send()

            @pl.when(jnp.logical_and(has_left, z + k < zeros))
            def _():
                hop(z + k, c, 1).wait_send()

        return carry

    lax.fori_loop(0, zeros, drain, 0)


def shards(zeros, models, *args):
    args = list(args)
    for i in (1, 4, 7, 10):
        args[i] = args[i].T
    for i in (12, 13):
        args[i] = args[i].reshape(1, -1)
    w_q, w_k, w_v, w_m = args[0], args[3], args[6], args[9]
    count = sum(-(-w.shape[0] // min(piece_rows, w.shape[0])) for w in (w_q, w_k, w_v, w_m)) + 1
    outs = [pltpu.VMEM((zeros * w.shape[0], w.shape[1]), w.dtype) for w in (w_q, w_k, w_v)]
    outs.append(pltpu.VMEM((w_m.shape[0], zeros * w_m.shape[1]), w_m.dtype))
    outs.append(pltpu.VMEM((zeros, models, 1, args[12].shape[1]), jnp.float32))
    final_query, final_key, final_value, final_mixed, norm = pl.pallas_call(
        functools.partial(merge_and_gather, zeros, models),
        out_shape=[jax.ShapeDtypeStruct(o.shape, o.dtype) for o in outs],
        in_specs=[pl.BlockSpec(memory_space=pl.ANY)] * 14,
        out_specs=[pl.BlockSpec(memory_space=pltpu.VMEM)] * 5,
        scratch_shapes=[pltpu.VMEM(a.shape, a.dtype) for a in args]
        + [
            pltpu.SemaphoreType.DMA((14,)),
            pltpu.SemaphoreType.DMA((2, zeros, count)),
            pltpu.SemaphoreType.DMA((zeros, count)),
            pltpu.SemaphoreType.DMA((models,)),
            pltpu.SemaphoreType.DMA((models,)),
        ],
        compiler_params=pltpu.CompilerParams(collective_id=0, has_side_effects=True),
    )(*args)
    serve_norm = norm.reshape(-1).astype(jnp.bfloat16)
    return final_query, final_key, final_value, final_mixed, serve_norm


def solution(mesh):
    placed = (
        P(("trial", "zero"), "model"),
        P(("trial", "zero"), None),
        P("trial", "model"),
        P(("trial", "zero"), "model"),
        P(("trial", "zero"), None),
        P("trial", "model"),
        P(("trial", "zero"), "model"),
        P(("trial", "zero"), None),
        P("trial", "model"),
        P(("trial", "model"), "zero"),
        P(("trial", "model"), None),
        P("trial", "zero"),
        P(("trial", "zero", "model")),
        P(("trial", "zero", "model")),
    )
    return jax.shard_map(
        functools.partial(shards, mesh.shape["zero"], mesh.shape["model"]),
        mesh=mesh,
        in_specs=placed,
        out_specs=(
            P("trial", "model"),
            P("trial", "model"),
            P("trial", "model"),
            P(("trial", "model"), None),
            P("trial"),
        ),
        check_vma=False,
    )
```

time: 132 us -> 103 us (0.78)
  Pallas kernels: 0 us -> 94.5 us
  blocking collectives: 65 us -> 0 us
  waiting for transfers between devices: 40.3 us -> 0 us
  between operations: 14.2 us -> 0.65 us
  matrix products: 4.8 us -> 0 us
    pallas_call x0 -> x1, Pallas kernels: none -> 94.5 us  [shards(): pl.pallas_call(functools.partial(merge_and_gather, zeros, models), out_sh...]
    all_gather x3 -> x0, blocking collectives: 65 us -> none  [the longest x1 23.1 us: shards(): lax.all_gather(narrow_key, 'zero', axis=0, tiled=True)]
    all_gather x2 -> x0, waiting for transfers between devices: 40.3 us -> none  [the longest x1 40.3 us: shards(): lax.all_gather(narrow_mixed, 'zero', axis=1, tiled=True)]
    dot_general x4 -> x0, matrix products: 4.8 us -> none  [the longest x1 2.2 us: shards(): jnp.dot(low_mixed, high_mixed, preferred_element_type=jnp.float32)]
    unnamed x24 -> x10, local copies, waits for them, and re-layouts: 6.78 us -> 6.12 us
  transfers between devices with their start and end apart: 2 -> 0, of which waited for: 1 -> 0; matrix products, arithmetic and copies ran while one was open for 2% -> 0% of each run, Pallas kernels for 0% -> 0%
where the time goes in v1:
time: 103 us
  Pallas kernels  94.5 us (92%)
  local copies, waits for them, and re-layouts  6.12 us (6%)
  other arithmetic  1.32 us (1%)
    pallas_call x1, Pallas kernels, shards(): pl.pallas_call(functools.partial(merge_and_gather, zeros, models), out_sh...  94.5 us
    unnamed x10, local copies, waits for them, and re-layouts  6.12 us

profile of v1, /device:TPU:0, one launch (start us, length us, event | category | flops | bytes accessed | tf_op | source)
XLA Modules:
  0.0 102.6 jit_solution(17694382416867145005)
XLA Ops:
  0.6 94.5 %shard_map.173 = (bf16[2048,512]{1,0:T(8,128)(2,1)}, bf16[2048,128]{1,0:T(8,128)(2,1)}, bf16[2048,128]{1,0:T(8,128)(2,1)}, bf16[512,2048]{1,0:T(8,128)(2,1)}, f32[4,4,1,128]{3,2,1,0:T(1,128)}) custom-call(bf16[512,512]{1,0:T(8,128)(2,1)} %refs_0_.1, bf16[32,512]{1,0:T(8,128)(2,1)} %bitcast.7, bf16[32,512]{1,0:T(8,128)(2,1)} %refs_2_.1, ...), custom_call_target="tpu_custom_call" | custom-call | tf_op jit(solution)/shard_map/pallas_call | solution.py:198
  95.2 1.3 %convert_reduce_fusion = bf16[4,4,128]{2,1,0:T(4,128)(2,1)} fusion(f32[4,4,1,128]{3,2,1,0:T(1,128)} %get-tuple-element.14), kind=kLoop, calls=%fused_computation | loop fusion | flops 2048 | bytes 12288 | tf_op jit(solution)/shard_map/convert_element_type | solution.py:213
  96.5 0.0 copy-start.2
  96.5 0.0 copy-start.1
  96.5 0.0 copy-start
  96.5 3.2 %copy.23 = bf16[2048,512]{1,0:T(8,128)(2,1)} copy(bf16[2048,512]{1,0:T(8,128)(2,1)} %get-tuple-element.20) | data formatting | bytes 4194304
  99.7 0.0 copy-done.2
  99.7 0.8 copy.24
  100.5 0.0 copy-done.1
  100.5 0.8 copy.25
  101.3 0.0 copy-done
  101.3 1.3 %copy.26 = bf16[512,2048]{1,0:T(8,128)(2,1)} copy(bf16[512,2048]{1,0:T(8,128)(2,1)S(1)} %copy-done) | data formatting | bytes 4194304
Async XLA Ops:
  96.5 3.2 %copy-start.2 = (bf16[2048,128]{1,0:T(8,128)(2,1)S(1)}, bf16[2048,128]{1,0:T(8,128)(2,1)}, u32[]{:S(2)}) copy-start(bf16[2048,128]{1,0:T(8,128)(2,1)} %get-tuple-element.21) | copy-start | bytes 1572868
  96.5 4.0 %copy-start.1 = (bf16[2048,128]{1,0:T(8,128)(2,1)S(1)}, bf16[2048,128]{1,0:T(8,128)(2,1)}, u32[]{:S(2)}) copy-start(bf16[2048,128]{1,0:T(8,128)(2,1)} %get-tuple-element.22) | copy-start | bytes 1572868
  96.5 4.8 %copy-start = (bf16[512,2048]{1,0:T(8,128)(2,1)S(1)}, bf16[512,2048]{1,0:T(8,128)(2,1)}, u32[]{:S(2)}) copy-start(bf16[512,2048]{1,0:T(8,128)(2,1)} %get-tuple-element.23) | copy-start | bytes 6291460

commit v2 on v1

--- a/solution.py
+++ b/solution.py
@@ -1,4 +1,5 @@
 import functools
+import math
 
 import jax
 import jax.numpy as jnp
@@ -10,6 +11,7 @@
 MESH = pl.DeviceIdType.MESH
 mix_rate = 2.0
 piece_rows = 128
+vmem_bytes = 67043328
 
 
 def merge_and_gather(zeros, models, *refs):
@@ -23,27 +25,27 @@
     m = lax.axis_index("model")
     has_right, has_left = z < zeros - 1, z > 0
 
+    barrier = pltpu.get_barrier_semaphore()
+
+    @pl.when(has_right)
+    def _():
+        pl.semaphore_signal(barrier, inc=1, device_id={"zero": z + 1}, device_id_type=MESH)
+
+    @pl.when(has_left)
+    def _():
+        pl.semaphore_signal(barrier, inc=1, device_id={"zero": z - 1}, device_id_type=MESH)
+
+    for d in range(1, models):
+        pl.semaphore_signal(
+            barrier, inc=1, device_id={"model": lax.rem(m + d, models)}, device_id_type=MESH
+        )
+
     loads = []
     for i in (1, 2, 0, 12, 13, 4, 5, 3, 7, 8, 6, 10, 11, 9):
         copy = pltpu.make_async_copy(refs[i], held[i], load_sem.at[i])
         copy.start()
         loads.append((i, copy))
     loads = dict(loads)
-
-    barrier = pltpu.get_barrier_semaphore()
-
-    @pl.when(has_right)
-    def _():
-        pl.semaphore_signal(barrier, inc=1, device_id={"zero": z + 1}, device_id_type=MESH)
-
-    @pl.when(has_left)
-    def _():
-        pl.semaphore_signal(barrier, inc=1, device_id={"zero": z - 1}, device_id_type=MESH)
-
-    for d in range(1, models):
-        pl.semaphore_signal(
-            barrier, inc=1, device_id={"model": lax.rem(m + d, models)}, device_id_type=MESH
-        )
 
     pieces = []
 
@@ -87,8 +89,28 @@
         def _():
             hop(z, c, 1).start()
 
+    def row(d):
+        return pltpu.make_async_remote_copy(
+            src_ref=out_n.at[z, m],
+            dst_ref=out_n.at[z, m],
+            send_sem=row_send.at[d],
+            recv_sem=row_recv.at[d],
+            device_id={"model": lax.rem(m + d, models)},
+            device_id_type=MESH,
+        )
+
+    def row_from(d):
+        sender = lax.rem(m + models - d, models)
+        return pltpu.make_async_remote_copy(
+            src_ref=out_n.at[z, sender],
+            dst_ref=out_n.at[z, sender],
+            send_sem=row_send.at[d],
+            recv_sem=row_recv.at[d],
+            device_id={"model": sender},
+            device_id_type=MESH,
+        )
+
     ready = []
-    waited = False
     for position, base, own in groups:
         for i in (1, 2, 0):
             loads[3 * position + i].wait()
@@ -103,40 +125,19 @@
             merged = w[first : first + size, :].astype(jnp.float32) + mix_rate * product
             view(z, base + j)[...] = merged.astype(out.dtype)
             ready.append(base + j)
+            if len(ready) == 2:
+                if ready[0] == 0:
+                    pl.semaphore_wait(
+                        barrier, models - 1 + has_right.astype(jnp.int32) + has_left.astype(jnp.int32)
+                    )
+                send_own(ready.pop(0))
         if position == 0:
             loads[12].wait()
             loads[13].wait()
             out_n[z, m] = held[12][...] + held[13][...]
-            pl.semaphore_wait(
-                barrier, models - 1 + has_right.astype(jnp.int32) + has_left.astype(jnp.int32)
-            )
-        while len(ready) > 1:
-            send_own(ready.pop(0))
+    for d in range(1, models):
+        row(d).start()
     send_own(ready.pop(0))
-
-    def row(d):
-        return pltpu.make_async_remote_copy(
-            src_ref=out_n.at[z, m],
-            dst_ref=out_n.at[z, m],
-            send_sem=row_send.at[d],
-            recv_sem=row_recv.at[d],
-            device_id={"model": lax.rem(m + d, models)},
-            device_id_type=MESH,
-        )
-
-    def row_from(d):
-        sender = lax.rem(m + models - d, models)
-        return pltpu.make_async_remote_copy(
-            src_ref=out_n.at[z, sender],
-            dst_ref=out_n.at[z, sender],
-            send_sem=row_send.at[d],
-            recv_sem=row_recv.at[d],
-            device_id={"model": sender},
-            device_id_type=MESH,
-        )
-
-    for d in range(1, models):
-        row(d).start()
     for d in range(1, models):
         row_from(d).wait_recv()
     send_own(count - 1)
@@ -182,6 +183,21 @@
         return carry
 
     lax.fori_loop(0, zeros, drain, 0)
+
+
+def write_out(*refs):
+    norm, wide, narrow, sem = refs[4], refs[10], refs[11], refs[12]
+    copies = [pltpu.make_async_copy(refs[i], refs[5 + i], sem.at[i]) for i in (0, 3, 1, 2)]
+    for copy in copies:
+        copy.start()
+    models = norm.shape[1]
+    for i in range(wide.shape[0]):
+        wide[i : i + 1, :] = norm[i // models, i % models]
+    narrow[...] = wide[...].astype(narrow.dtype)
+    copies.append(pltpu.make_async_copy(narrow, refs[9], sem.at[4]))
+    copies[-1].start()
+    for copy in copies:
+        copy.wait()
 
 
 def shards(zeros, models, *args):
@@ -195,11 +211,11 @@
     outs = [pltpu.VMEM((zeros * w.shape[0], w.shape[1]), w.dtype) for w in (w_q, w_k, w_v)]
     outs.append(pltpu.VMEM((w_m.shape[0], zeros * w_m.shape[1]), w_m.dtype))
     outs.append(pltpu.VMEM((zeros, models, 1, args[12].shape[1]), jnp.float32))
+    held_bytes = sum(math.prod(o.shape) * jnp.dtype(o.dtype).itemsize for o in outs)
     final_query, final_key, final_value, final_mixed, norm = pl.pallas_call(
         functools.partial(merge_and_gather, zeros, models),
-        out_shape=[jax.ShapeDtypeStruct(o.shape, o.dtype) for o in outs],
-        in_specs=[pl.BlockSpec(memory_space=pl.ANY)] * 14,
-        out_specs=[pl.BlockSpec(memory_space=pltpu.VMEM)] * 5,
+        out_shape=outs,
+        in_specs=[pl.BlockSpec(memory_space=pltpu.HBM)] * 14,
         scratch_shapes=[pltpu.VMEM(a.shape, a.dtype) for a in args]
         + [
             pltpu.SemaphoreType.DMA((14,)),
@@ -208,10 +224,28 @@
             pltpu.SemaphoreType.DMA((models,)),
             pltpu.SemaphoreType.DMA((models,)),
         ],
-        compiler_params=pltpu.CompilerParams(collective_id=0, has_side_effects=True),
+        compiler_params=pltpu.CompilerParams(
+            collective_id=0,
+            has_side_effects=True,
+            vmem_limit_bytes=vmem_bytes - held_bytes - 128 * 1024,
+        ),
     )(*args)
-    serve_norm = norm.reshape(-1).astype(jnp.bfloat16)
-    return final_query, final_key, final_value, final_mixed, serve_norm
+    gathered = [final_query, final_key, final_value, final_mixed]
+    gains = norm.shape[0] * norm.shape[1], norm.shape[3]
+    *finals, serve_norm = pl.pallas_call(
+        write_out,
+        out_shape=[jax.ShapeDtypeStruct(g.shape, g.dtype) for g in gathered]
+        + [jax.ShapeDtypeStruct(gains, jnp.bfloat16)],
+        in_specs=[pl.BlockSpec(memory_space=pltpu.VMEM)] * 5,
+        out_specs=[pl.BlockSpec(memory_space=pltpu.HBM)] * 5,
+        scratch_shapes=[
+            pltpu.VMEM(gains, jnp.float32),
+            pltpu.VMEM(gains, jnp.bfloat16),
+            pltpu.SemaphoreType.DMA((5,)),
+        ],
+        compiler_params=pltpu.CompilerParams(vmem_limit_bytes=16 * 1024 * 1024),
+    )(*gathered, norm)
+    return (*finals, serve_norm.reshape(-1))
 
 
 def solution(mesh):

time: 103 us -> 95.4 us (0.926)
  local copies, waits for them, and re-layouts: 6.12 us -> 0 us
  other arithmetic: 1.32 us -> 0 us
    unnamed x10 -> x0, local copies, waits for them, and re-layouts: 6.12 us -> none
    pallas_call x0 -> x1, Pallas kernels: none -> 2.38 us  [shards(): pl.pallas_call(write_out, out_shape=[jax.ShapeDtypeStruct(g.shape, g.dtyp...]
    pallas_call x1, Pallas kernels: 94.5 us -> 92.2 us  [shards(): pl.pallas_call(functools.partial(merge_and_gather, zeros, models), out_sh...]
    convert_element_type x1 -> x0, other arithmetic: 1.32 us -> none  [shards(): serve_norm = norm.reshape(-1).astype(jnp.bfloat16)]
where the time goes in v2:
time: 95.4 us; the launch traced here: 95.2 us
  Pallas kernels  94.6 us (99%)
    pallas_call x1, Pallas kernels, shards(): pl.pallas_call(functools.partial(merge_and_gather, zeros, models), out_sh...  92.2 us
    pallas_call x1, Pallas kernels, shards(): pl.pallas_call(write_out, out_shape=[jax.ShapeDtypeStruct(g.shape, g.dtyp...  2.38 us

profile of v2, /device:TPU:0, one launch (start us, length us, event | category | flops | bytes accessed | tf_op | source)
XLA Modules:
  0.0 95.2 jit_solution(9074155720656963359)
XLA Ops:
  0.6 92.2 %shard_map.173 = (bf16[2048,512]{1,0:T(8,128)(2,1)S(1)}, bf16[2048,128]{1,0:T(8,128)(2,1)S(1)}, bf16[2048,128]{1,0:T(8,128)(2,1)S(1)}, bf16[512,2048]{1,0:T(8,128)(2,1)S(1)}, f32[4,4,1,128]{3,2,1,0:T(1,128)S(1)}) custom-call(bf16[512,512]{1,0:T(8,128)(2,1)} %refs_0_.1, bf16[32,512]{1,0:T(8,128)(2,1)} %bitcast.7, bf16[32,512]{1,0:T(8,128)(2,1)} %refs_2_.1, ...), custom_call_target="tpu_custom_call" | custom-call | tf_op jit(solution)/shard_map/pallas_call | solution.py:215
  92.8 2.4 %shard_map.174 = (bf16[2048,512]{1,0:T(8,128)(2,1)}, bf16[2048,128]{1,0:T(8,128)(2,1)}, bf16[2048,128]{1,0:T(8,128)(2,1)}, bf16[512,2048]{1,0:T(8,128)(2,1)}, bf16[16,128]{1,0:T(8,128)(2,1)}) custom-call(bf16[2048,512]{1,0:T(8,128)(2,1)S(1)} %get-tuple-element.15.refs_0_, bf16[2048,128]{1,0:T(8,128)(2,1)S(1)} %get-tuple-element.16.refs_1_, ...), custom_call_target="tpu_custom_call" | custom-call | tf_op jit(solution)/shard_map/pallas_call | solution.py:235

commit v3 on v2

--- a/solution.py
+++ b/solution.py
@@ -10,7 +10,7 @@
 
 MESH = pl.DeviceIdType.MESH
 mix_rate = 2.0
-piece_rows = 128
+piece_rows = 512
 vmem_bytes = 67043328
 
 

time: 95.4 us -> 94 us (0.985)
  Pallas kernels: 94.6 us -> 93.2 us
    pallas_call x1, Pallas kernels: 92.2 us -> 90.8 us  [shards(): pl.pallas_call(functools.partial(merge_and_gather, zeros, models), out_sh...]
where the time goes in v3:
time: 94 us; the launch traced here: 93.8 us
  Pallas kernels  93.2 us (99%)
    pallas_call x1, Pallas kernels, shards(): pl.pallas_call(functools.partial(merge_and_gather, zeros, models), out_sh...  90.8 us
    pallas_call x1, Pallas kernels, shards(): pl.pallas_call(write_out, out_shape=[jax.ShapeDtypeStruct(g.shape, g.dtyp...  2.38 us

profile of v3, /device:TPU:0, one launch (start us, length us, event | category | flops | bytes accessed | tf_op | source)
XLA Modules:
  0.0 93.8 jit_solution(4878435851550070565)
XLA Ops:
  0.6 90.8 %shard_map.173 = (bf16[2048,512]{1,0:T(8,128)(2,1)S(1)}, bf16[2048,128]{1,0:T(8,128)(2,1)S(1)}, bf16[2048,128]{1,0:T(8,128)(2,1)S(1)}, bf16[512,2048]{1,0:T(8,128)(2,1)S(1)}, f32[4,4,1,128]{3,2,1,0:T(1,128)S(1)}) custom-call(bf16[512,512]{1,0:T(8,128)(2,1)} %refs_0_.1, bf16[32,512]{1,0:T(8,128)(2,1)} %bitcast.7, bf16[32,512]{1,0:T(8,128)(2,1)} %refs_2_.1, ...), custom_call_target="tpu_custom_call" | custom-call | tf_op jit(solution)/shard_map/pallas_call | solution.py:215
  91.4 2.4 %shard_map.174 = (bf16[2048,512]{1,0:T(8,128)(2,1)}, bf16[2048,128]{1,0:T(8,128)(2,1)}, bf16[2048,128]{1,0:T(8,128)(2,1)}, bf16[512,2048]{1,0:T(8,128)(2,1)}, bf16[16,128]{1,0:T(8,128)(2,1)}) custom-call(bf16[2048,512]{1,0:T(8,128)(2,1)S(1)} %get-tuple-element.15.refs_0_, bf16[2048,128]{1,0:T(8,128)(2,1)S(1)} %get-tuple-element.16.refs_1_, ...), custom_call_target="tpu_custom_call" | custom-call | tf_op jit(solution)/shard_map/pallas_call | solution.py:235

commit v4 on v3

--- a/solution.py
+++ b/solution.py
@@ -19,7 +19,7 @@
     train, step = refs[12:14]
     out_q, out_k, out_v, out_m, out_n = refs[14:19]
     held = refs[19:33]
-    load_sem, send_sem, recv_sem, row_send, row_recv = refs[33:]
+    load_sem, send_sem, recv_sem, row_send, row_recv, right_in, left_send, rows = refs[33:]
 
     z = lax.axis_index("zero")
     m = lax.axis_index("model")
@@ -31,14 +31,12 @@
     def _():
         pl.semaphore_signal(barrier, inc=1, device_id={"zero": z + 1}, device_id_type=MESH)
 
-    @pl.when(has_left)
-    def _():
-        pl.semaphore_signal(barrier, inc=1, device_id={"zero": z - 1}, device_id_type=MESH)
-
-    for d in range(1, models):
-        pl.semaphore_signal(
-            barrier, inc=1, device_id={"model": lax.rem(m + d, models)}, device_id_type=MESH
-        )
+    @pl.when(z == 0)
+    def _():
+        for d in range(1, models):
+            pl.semaphore_signal(
+                barrier, inc=1, device_id={"model": lax.rem(m + d, models)}, device_id_type=MESH
+            )
 
     loads = []
     for i in (1, 2, 0, 12, 13, 4, 5, 3, 7, 8, 6, 10, 11, 9):
@@ -52,6 +50,8 @@
     def rows_of(out, w):
         rows = w.shape[0]
         size = min(piece_rows, rows)
+        if out is out_q and rows > 128:
+            return [(out, w, 0, 128), (out, w, 128, rows - 128)]
         return [(out, w, first, size) for first in range(0, rows, size)]
 
     groups = []
@@ -59,16 +59,14 @@
         own = rows_of(out, w)
         groups.append((position, len(pieces), own))
         pieces += own
-    count = len(pieces) + 1
+    count = len(pieces)
 
     def view(shard, c):
-        if c == count - 1:
-            return out_n.at[shard]
         out, w, first, size = pieces[c]
         rows, columns = w.shape
         if out is out_m:
             return out.at[pl.ds(first, size), pl.ds(pl.multiple_of(shard * columns, columns), columns)]
-        return out.at[pl.ds(pl.multiple_of(shard * rows + first, size), size), :]
+        return out.at[pl.ds(pl.multiple_of(shard * rows + first, 128), size), :]
 
     def hop(shard, c, way):
         return pltpu.make_async_remote_copy(
@@ -81,34 +79,50 @@
         )
 
     def send_own(c):
+        @pl.when(has_left)
+        def _():
+            hop(z, c, 1).start()
+
         @pl.when(has_right)
         def _():
+            if c == 0:
+                pl.semaphore_wait(right_in, 1)
             hop(z, c, 0).start()
 
-        @pl.when(has_left)
-        def _():
-            hop(z, c, 1).start()
-
-    def row(d):
+    def row_left(shard):
         return pltpu.make_async_remote_copy(
-            src_ref=out_n.at[z, m],
-            dst_ref=out_n.at[z, m],
+            src_ref=rows.at[shard],
+            dst_ref=rows.at[shard],
+            send_sem=left_send.at[0, shard],
+            recv_sem=left_send.at[1, shard],
+            device_id={"zero": z - 1},
+            device_id_type=MESH,
+        )
+
+    def column(d, sender):
+        return pltpu.make_async_remote_copy(
+            src_ref=out_n.at[:, sender],
+            dst_ref=out_n.at[:, sender],
             send_sem=row_send.at[d],
             recv_sem=row_recv.at[d],
             device_id={"model": lax.rem(m + d, models)},
             device_id_type=MESH,
         )
 
-    def row_from(d):
-        sender = lax.rem(m + models - d, models)
+    def norm_right():
         return pltpu.make_async_remote_copy(
-            src_ref=out_n.at[z, sender],
-            dst_ref=out_n.at[z, sender],
-            send_sem=row_send.at[d],
-            recv_sem=row_recv.at[d],
-            device_id={"model": sender},
+            src_ref=out_n,
+            dst_ref=out_n,
+            send_sem=row_send.at[0],
+            recv_sem=row_recv.at[0],
+            device_id={"zero": z + 1},
             device_id_type=MESH,
         )
+
+    @pl.when(has_left)
+    def _():
+        pl.semaphore_wait(barrier, 1)
+        pl.semaphore_signal(right_in, inc=1, device_id={"zero": z - 1}, device_id_type=MESH)
 
     ready = []
     for position, base, own in groups:
@@ -125,25 +139,42 @@
             merged = w[first : first + size, :].astype(jnp.float32) + mix_rate * product
             view(z, base + j)[...] = merged.astype(out.dtype)
             ready.append(base + j)
-            if len(ready) == 2:
-                if ready[0] == 0:
-                    pl.semaphore_wait(
-                        barrier, models - 1 + has_right.astype(jnp.int32) + has_left.astype(jnp.int32)
-                    )
+            if len(ready) == (2 if base + j != 0 else 1):
                 send_own(ready.pop(0))
         if position == 0:
             loads[12].wait()
             loads[13].wait()
-            out_n[z, m] = held[12][...] + held[13][...]
-    for d in range(1, models):
-        row(d).start()
+            rows[z] = held[12][...] + held[13][...]
+
+            @pl.when(has_left)
+            def _():
+                row_left(z).start()
     send_own(ready.pop(0))
-    for d in range(1, models):
-        row_from(d).wait_recv()
-    send_own(count - 1)
 
     def pass_on(k, carry):
         from_left, from_right = z - 1 - k, z + 1 + k
+
+        @pl.when(from_right < zeros)
+        def _():
+            row_left(from_right).wait_recv()
+
+            @pl.when(has_left)
+            def _():
+                row_left(from_right).start()
+
+        @pl.when(jnp.logical_and(z == 0, k == zeros - 2))
+        def _():
+            for i in range(zeros):
+                out_n[i, m] = rows[i]
+            pl.semaphore_wait(barrier, models - 1)
+            for d in range(1, models):
+                column(d, m).start()
+            for d in range(1, models):
+                column(d, lax.rem(m + models - d, models)).wait_recv()
+            for d in range(1, models):
+                column(d, m).wait_send()
+            norm_right().start()
+
         for c in range(count):
 
             @pl.when(from_left >= 0)
@@ -166,10 +197,24 @@
 
     lax.fori_loop(0, zeros - 1, pass_on, 0)
 
-    for d in range(1, models):
-        row(d).wait_send()
+    @pl.when(has_left)
+    def _():
+        norm_right().wait_recv()
+
+        @pl.when(has_right)
+        def _():
+            norm_right().start()
+
+    @pl.when(has_right)
+    def _():
+        norm_right().wait_send()
+
 
     def drain(k, carry):
+        @pl.when(jnp.logical_and(has_left, z + k < zeros))
+        def _():
+            row_left(z + k).wait_send()
+
         for c in range(count):
 
             @pl.when(jnp.logical_and(has_right, z - k >= 0))
@@ -223,6 +268,9 @@
             pltpu.SemaphoreType.DMA((zeros, count)),
             pltpu.SemaphoreType.DMA((models,)),
             pltpu.SemaphoreType.DMA((models,)),
+            pltpu.SemaphoreType.REGULAR,
+            pltpu.SemaphoreType.DMA((2, zeros)),
+            pltpu.VMEM((zeros, 1, args[12].shape[1]), jnp.float32),
         ],
         compiler_params=pltpu.CompilerParams(
             collective_id=0,

time: 94 us -> 93.4 us (level)
  no operation moved by 1% of the time
where the time goes in v4:
time: 93.4 us; the launch traced here: 93.2 us
  Pallas kernels  92.6 us (99%)
    pallas_call x1, Pallas kernels, shards(): pl.pallas_call(functools.partial(merge_and_gather, zeros, models), out_sh...  90.2 us
    pallas_call x1, Pallas kernels, shards(): pl.pallas_call(write_out, out_shape=[jax.ShapeDtypeStruct(g.shape, g.dtyp...  2.38 us

profile of v4, /device:TPU:0, one launch (start us, length us, event | category | flops | bytes accessed | tf_op | source)
XLA Modules:
  0.0 93.2 jit_solution(5853651029436058948)
XLA Ops:
  0.6 90.2 %shard_map.173 = (bf16[2048,512]{1,0:T(8,128)(2,1)S(1)}, bf16[2048,128]{1,0:T(8,128)(2,1)S(1)}, bf16[2048,128]{1,0:T(8,128)(2,1)S(1)}, bf16[512,2048]{1,0:T(8,128)(2,1)S(1)}, f32[4,4,1,128]{3,2,1,0:T(1,128)S(1)}) custom-call(bf16[512,512]{1,0:T(8,128)(2,1)} %refs_0_.1, bf16[32,512]{1,0:T(8,128)(2,1)} %bitcast.7, bf16[32,512]{1,0:T(8,128)(2,1)} %refs_2_.1, ...), custom_call_target="tpu_custom_call" | custom-call | tf_op jit(solution)/shard_map/pallas_call | solution.py:260
  90.8 2.4 %shard_map.174 = (bf16[2048,512]{1,0:T(8,128)(2,1)}, bf16[2048,128]{1,0:T(8,128)(2,1)}, bf16[2048,128]{1,0:T(8,128)(2,1)}, bf16[512,2048]{1,0:T(8,128)(2,1)}, bf16[16,128]{1,0:T(8,128)(2,1)}) custom-call(bf16[2048,512]{1,0:T(8,128)(2,1)S(1)} %get-tuple-element.15.refs_0_, bf16[2048,128]{1,0:T(8,128)(2,1)S(1)} %get-tuple-element.16.refs_1_, ...), custom_call_target="tpu_custom_call" | custom-call | tf_op jit(solution)/shard_map/pallas_call | solution.py:283

commit v5 on v4

--- a/solution.py
+++ b/solution.py
@@ -39,7 +39,7 @@
             )
 
     loads = []
-    for i in (1, 2, 0, 12, 13, 4, 5, 3, 7, 8, 6, 10, 11, 9):
+    for i in (4, 5, 3, 1, 2, 0, 12, 13, 7, 8, 6, 10, 11, 9):
         copy = pltpu.make_async_copy(refs[i], held[i], load_sem.at[i])
         copy.start()
         loads.append((i, copy))
@@ -50,12 +50,10 @@
     def rows_of(out, w):
         rows = w.shape[0]
         size = min(piece_rows, rows)
-        if out is out_q and rows > 128:
-            return [(out, w, 0, 128), (out, w, 128, rows - 128)]
         return [(out, w, first, size) for first in range(0, rows, size)]
 
     groups = []
-    for position, (out, w) in enumerate(((out_q, w_q), (out_k, w_k), (out_v, w_v), (out_m, w_m))):
+    for position, out, w in ((1, out_k, w_k), (0, out_q, w_q), (2, out_v, w_v), (3, out_m, w_m)):
         own = rows_of(out, w)
         groups.append((position, len(pieces), own))
         pieces += own
@@ -252,7 +250,7 @@
     for i in (12, 13):
         args[i] = args[i].reshape(1, -1)
     w_q, w_k, w_v, w_m = args[0], args[3], args[6], args[9]
-    count = sum(-(-w.shape[0] // min(piece_rows, w.shape[0])) for w in (w_q, w_k, w_v, w_m)) + 1
+    count = sum(-(-w.shape[0] // min(piece_rows, w.shape[0])) for w in (w_q, w_k, w_v, w_m))
     outs = [pltpu.VMEM((zeros * w.shape[0], w.shape[1]), w.dtype) for w in (w_q, w_k, w_v)]
     outs.append(pltpu.VMEM((w_m.shape[0], zeros * w_m.shape[1]), w_m.dtype))
     outs.append(pltpu.VMEM((zeros, models, 1, args[12].shape[1]), jnp.float32))

time: 93.4 us -> 93.1 us (level)
  no operation moved by 1% of the time
where the time goes in v5:
time: 93.1 us; the launch traced here: 93 us
  Pallas kernels  92.4 us (99%)
    pallas_call x1, Pallas kernels, shards(): pl.pallas_call(functools.partial(merge_and_gather, zeros, models), out_sh...  90 us
    pallas_call x1, Pallas kernels, shards(): pl.pallas_call(write_out, out_shape=[jax.ShapeDtypeStruct(g.shape, g.dtyp...  2.38 us

profile of v5, /device:TPU:0, one launch (start us, length us, event | category | flops | bytes accessed | tf_op | source)
XLA Modules:
  0.0 93.0 jit_solution(945729468247584133)
XLA Ops:
  0.6 90.0 %shard_map.173 = (bf16[2048,512]{1,0:T(8,128)(2,1)S(1)}, bf16[2048,128]{1,0:T(8,128)(2,1)S(1)}, bf16[2048,128]{1,0:T(8,128)(2,1)S(1)}, bf16[512,2048]{1,0:T(8,128)(2,1)S(1)}, f32[4,4,1,128]{3,2,1,0:T(1,128)S(1)}) custom-call(bf16[512,512]{1,0:T(8,128)(2,1)} %refs_0_.1, bf16[32,512]{1,0:T(8,128)(2,1)} %bitcast.7, bf16[32,512]{1,0:T(8,128)(2,1)} %refs_2_.1, ...), custom_call_target="tpu_custom_call" | custom-call | tf_op jit(solution)/shard_map/pallas_call | solution.py:258
  90.6 2.4 %shard_map.174 = (bf16[2048,512]{1,0:T(8,128)(2,1)}, bf16[2048,128]{1,0:T(8,128)(2,1)}, bf16[2048,128]{1,0:T(8,128)(2,1)}, bf16[512,2048]{1,0:T(8,128)(2,1)}, bf16[16,128]{1,0:T(8,128)(2,1)}) custom-call(bf16[2048,512]{1,0:T(8,128)(2,1)S(1)} %get-tuple-element.15.refs_0_, bf16[2048,128]{1,0:T(8,128)(2,1)S(1)} %get-tuple-element.16.refs_1_, ...), custom_call_target="tpu_custom_call" | custom-call | tf_op jit(solution)/shard_map/pallas_call | solution.py:281
